TPU v7x, 256 devices: a whole 4x4x8 slice. The times are simulated.
256 devices in a mesh: layer: 4 (over z_lo, core), feat: 64 (over y, z_hi, x).
Axes of the slice: x: 4, y: 4, z: 8 (z_hi: 4, z_lo: 2; z = z_hi * 2 + z_lo), core: 2. Of those that a mesh axis runs over, the one named last changes fastest.
Arguments:
- activations: bfloat16 [512, 4, 2304], P('feat', 'layer'), may hold values from -6 to 6
- enc_weight: bfloat16 [4, 2304, 65536], P('layer', None, 'feat'), may hold values from -0.0625 to 0.0625
- dec_weight: bfloat16 [4, 65536, 2304], P('layer', 'feat'), may hold values from -0.03125 to 0.03125
- enc_bias: float32 [65536], P('feat'), may hold values from -3 to 3
- threshold: float32 [65536], P('feat'), may hold values from 0.1 to 1
- dec_bias: float32 [4, 2304], P('layer'), may hold values from -3 to 3
- token_mask: int32 [512], replicated, may hold values 0 or 1
Outputs:
- squared_error: float32 [512, 4], P('feat', 'layer')
- latent_grad: float32 [512, 65536], P(None, 'feat')
- input_grad: bfloat16 [512, 4, 2304], P('feat', 'layer')
All inputs are finite; a program needn't handle non-finite values.
Results may differ from a plain program's by a relative error of at most 0.015.
Values may be sent and summed in bfloat16 or wider, within the bound.
A program may use at most 64 MiB of HBM per device.

v0:
```python
import jax
import jax.numpy as jnp
from jax import lax
from jax.sharding import Mesh
from jax.sharding import PartitionSpec as P

FEAT = ("feat_0", "feat_1", "feat_2")
jump_scale = 0.25


def split_up(array, dim, length):
    before, after = (array.shape[:dim], array.shape[dim + 1 :])
    return jnp.moveaxis(array.reshape(*before, length, -1, *after), dim, 0)


def sent_and_summed(array, axis, dim):
    length = lax.axis_size(axis)
    parts = lax.all_to_all(split_up(array, dim, length), axis, 0, 0, tiled=True)
    return jnp.sum(parts, axis=0)


def sum_by_axis(array, axes, dim):
    far, near = axes
    parts = split_up(array, dim, lax.axis_size(far))
    nearer = sent_and_summed(parts, near, dim + 1)
    arrived = lax.all_to_all(nearer, far, split_axis=0, concat_axis=0, tiled=True)
    return arrived.sum(axis=0)


def shards(activations, enc_weight, dec_weight, enc_bias, threshold, dec_bias, token_mask):
    tok_dev = activations.shape[0]
    partial_value = jnp.einsum(
        "tld,ldf->tf",
        lax.all_gather(activations, FEAT, axis=0, tiled=True),
        enc_weight,
        preferred_element_type=jnp.float32,
    )
    preact = lax.psum(partial_value.astype(jnp.bfloat16), "layer").astype(jnp.float32) + enc_bias
    gating = jax.nn.sigmoid((preact - threshold) / jump_scale)
    latent = (preact * gating).astype(jnp.bfloat16)
    gate_slope = gating + preact * gating * (1.0 - gating) / jump_scale
    first_row = lax.axis_index(FEAT) * tok_dev
    rows = latent
    rebuilt = sum_by_axis(
        jnp.einsum("tf,lfd->tld", rows, dec_weight, preferred_element_type=jnp.float32),
        (("feat_0", "feat_1"), "feat_2"),
        0,
    )
    own_mask = lax.dynamic_slice_in_dim(token_mask, first_row, tok_dev, 0).astype(jnp.float32)[
        :, None, None
    ]
    error = own_mask * (rebuilt + dec_bias[None, :, :] - activations.astype(jnp.float32))
    grad_part = jnp.einsum(
        "tld,lfd->tf",
        lax.all_gather(error.astype(jnp.bfloat16), FEAT, axis=0, tiled=True),
        dec_weight,
        preferred_element_type=jnp.float32,
    )
    squared_error = jnp.mean(error * error, axis=-1)
    latent_grad = lax.psum(grad_part.astype(jnp.bfloat16), "layer").astype(jnp.float32)
    preact_grad = (latent_grad * gate_slope).astype(jnp.bfloat16)
    rows = preact_grad
    grad_terms = sum_by_axis(
        jnp.einsum("tf,ldf->tld", rows, enc_weight, preferred_element_type=jnp.float32),
        (("feat_0", "feat_1"), "feat_2"),
        0,
    )
    input_grad = (grad_terms - error).astype(jnp.bfloat16)
    return (squared_error, latent_grad, input_grad)


def solution(mesh):
    finer = Mesh(
        mesh.devices.reshape(mesh.shape["layer"], 4, 4, 4), ("layer", "feat_0", "feat_1", "feat_2")
    )
    return jax.shard_map(
        shards,
        mesh=finer,
        in_specs=(
            P(FEAT, "layer", None),
            P("layer", None, FEAT),
            P("layer", FEAT, None),
            P(FEAT),
            P(FEAT),
            P("layer", None),
            P(),
        ),
        out_specs=(P(FEAT, "layer"), P(None, FEAT), P(FEAT, "layer", None)),
        check_vma=False,
    )
```

profile of v0, /device:TPU:32, one launch (start us, length us, event | category | flops | bytes accessed | tf_op | source)
XLA Modules:
  0.0 498.0 jit_solution(7002110068138016690)
XLA Ops:
  7.2 0.7 all-gather.3.cloned.1.call-update
  8.0 84.0 %all-gather.3.cloned.1.call-done = bf16[512,1,2304]{2,0,1:T(8,128)(2,1)} async-done(((bf16[8,1,2304]{2,0,1:T(8,128)(2,1)}), bf16[512,1,2304]{2,0,1:T(8,128)(2,1)}) %all-gather.3.cloned.1.call-update) | async-done | bytes 2359312 | tf_op jit(solution)/shard_map/all_gather | solution.py:34
  91.9 6.6 %fusion.10 = bf16[512,1024]{1,0:T(8,128)(2,1)} fusion(bf16[1,2304,1024]{2,1,0:T(8,128)(2,1)} %param.8, bf16[512,1,2304]{2,0,1:T(8,128)(2,1)} %all-gather.3.cloned.1.call-done), kind=kOutput, calls=%fused_computation.15 | convolution fusion | flops 2416443392 | bytes 8126464 | tf_op jit(solution)/shard_map/tld,ldf->tf/dot_general | solution.py:32
  98.6 44.8 %all-reduce.3.cloned.1.call-done = bf16[512,1024]{1,0:T(8,128)(2,1)} async-done(((bf16[512,1024]{1,0:T(8,128)(2,1)}), bf16[512,1024]{1,0:T(8,128)(2,1)}) %all-reduce.3.cloned.1.call-update) | async-done | bytes 1048592 | tf_op jit(solution)/shard_map/psum | solution.py:38
  143.4 1.9 fusion.9
  145.3 4.9 convolution_bitcast_fusion.1
  150.2 0.4 copy.10
  150.6 58.9 %all_to_all.20 = f32[4,16,8,1,2304]{4,2,1,3,0:T(8,128)} all-to-all(f32[4,16,8,1,2304]{4,2,1,3,0:T(8,128)S(1)} %copy.10), channel_id=1, replica_groups=mesh['layer'=4,'feat_0'=4,'feat_1'=4,'feat_2'=4] {'feat_2'}, dimensions={0} | all-to-all | bytes 9437184 | tf_op jit(solution)/shard_map/all_to_all | solution.py:18
  209.6 3.7 reduce_sum.53
  213.3 9.2 %all-to-all-start.1 = ((f32[16,8,1,2304]{3,1,2,0:T(8,128)}), f32[16,8,1,2304]{3,1,2,0:T(8,128)S(1)}, u32[]{:S(2)}, u32[]{:S(2)}) async-start(f32[16,8,1,2304]{3,1,2,0:T(8,128)} %bitcast.8), calls=%async_computation.1 | async-start | bytes 2359296 | tf_op jit(solution)/shard_map/all_to_all | solution.py:26
  222.6 0.8 dynamic-slice_convert_fusion
  223.4 31.0 %all-to-all-done.1 = f32[16,8,1,2304]{3,1,2,0:T(8,128)S(1)} async-done(((f32[16,8,1,2304]{3,1,2,0:T(8,128)}), f32[16,8,1,2304]{3,1,2,0:T(8,128)S(1)}, u32[]{:S(2)}, u32[]{:S(2)}) %all-to-all-start.1) | async-done | bytes 1179680 | tf_op jit(solution)/shard_map/all_to_all | solution.py:26
  254.5 0.7 fusion.23
  255.5 71.8 %all-gather.5.cloned.1.call-done = bf16[512,1,2304]{2,0,1:T(8,128)(2,1)} async-done(((bf16[8,1,2304]{2,0,1:T(8,128)(2,1)}), bf16[512,1,2304]{2,0,1:T(8,128)(2,1)}) %all-gather.5.cloned.1.call-update) | async-done | bytes 2359312 | tf_op jit(solution)/shard_map/all_gather | solution.py:55
  327.3 6.7 %fusion.15 = bf16[512,1024]{1,0:T(8,128)(2,1)} fusion(bf16[1,1024,2304]{2,1,0:T(8,128)(2,1)} %param.9, bf16[512,1,2304]{2,0,1:T(8,128)(2,1)} %all-gather.5.cloned.1.call-done), kind=kOutput, calls=%fused_computation.16 | convolution fusion | flops 2416443392 | bytes 8126464 | tf_op jit(solution)/shard_map/tld,lfd->tf/dot_general | solution.py:53
  333.9 44.7 %all-reduce.5.cloned.1.call-done = bf16[512,1024]{1,0:T(8,128)(2,1)} async-done(((bf16[512,1024]{1,0:T(8,128)(2,1)}), bf16[512,1024]{1,0:T(8,128)(2,1)}) %all-reduce.5.cloned.1.call-update) | async-done | bytes 1048592 | tf_op jit(solution)/shard_map/psum | solution.py:60
  378.7 3.6 multiply_convert_fusion
  382.3 5.0 %convolution_bitcast_fusion = f32[4,16,8,1,2304]{4,2,0,1,3:T(8,128)S(1)} fusion(bf16[16,4,8,1024]{3,2,1,0:T(8,128)(2,1)S(1)} %bitcast.65, bf16[1,2304,1024]{2,1,0:T(8,128)(2,1)} %param.8), kind=kOutput, calls=%fused_computation | convolution fusion | flops 2415919104 | bytes 10485760 | tf_op jit(solution)/shard_map/tf,ldf->tld/dot_general | solution.py:64
  387.3 0.4 copy.11
  387.7 58.9 %all_to_all.21 = f32[4,16,8,1,2304]{4,2,1,3,0:T(8,128)} all-to-all(f32[4,16,8,1,2304]{4,2,1,3,0:T(8,128)S(1)} %copy.11), channel_id=1, replica_groups=mesh['layer'=4,'feat_0'=4,'feat_1'=4,'feat_2'=4] {'feat_2'}, dimensions={0} | all-to-all | bytes 9437184 | tf_op jit(solution)/shard_map/all_to_all | solution.py:18
  446.6 2.7 reduce_sum.58
  449.4 40.7 %all_to_all.22 = f32[16,8,1,2304]{3,1,2,0:T(8,128)S(1)} all-to-all(f32[16,8,1,2304]{3,1,2,0:T(8,128)S(1)} %bitcast.64), channel_id=1, replica_groups=mesh['layer'=4,'feat_0'=4,'feat_1'=4,'feat_2'=4] {'feat_0','feat_1'}, dimensions={0} | all-to-all | bytes 2359296 | tf_op jit(solution)/shard_map/all_to_all | solution.py:26
  490.1 0.8 fusion.20
  490.9 0.5 multiply_bitcast_fusion
  (20 shorter events, 0.6 us)
Async XLA Ops:
  7.2 84.8 %all-gather.3.cloned.1.call-start = ((), (), s32[]{:S(2)}) async-start(), calls=%async_computation.4 | async-start | bytes 2396160 | tf_op jit(solution)/shard_map/all_gather | solution.py:34
  7.9 135.5 %copy-start.2 = (f32[1024]{0:T(1024)S(1)}, f32[1024]{0:T(1024)}, u32[]{:S(2)}) copy-start(f32[1024]{0:T(1024)} %param.11) | copy-start | bytes 12292
  7.9 135.5 %copy-start.3 = (f32[1024]{0:T(1024)S(1)}, f32[1024]{0:T(1024)}, u32[]{:S(2)}) copy-start(f32[1024]{0:T(1024)} %param.10) | copy-start | bytes 12292
  7.9 135.4 %all-reduce.3.cloned.1.call-start = ((), (), s32[]{:S(2)}) async-start(), calls=%async_computation.5 | async-start | bytes 2097152 | tf_op jit(solution)/shard_map/psum | solution.py:38
  213.3 9.3 %copy-start.4 = (f32[1,2304]{1,0:T(1,128)S(1)}, f32[1,2304]{1,0:T(1,128)}, u32[]{:S(2)}) copy-start(f32[1,2304]{1,0:T(1,128)} %param.12) | copy-start | bytes 27652
  213.3 41.2 %copy-start.1 = (bf16[8,1,2304]{2,0,1:T(8,128)(2,1)S(1)}, bf16[8,1,2304]{2,0,1:T(8,128)(2,1)}, u32[]{:S(2)}) copy-start(bf16[8,1,2304]{2,0,1:T(8,128)(2,1)} %param.7) | copy-start | bytes 110596
  213.3 41.1 %all-to-all-start.1 = ((f32[16,8,1,2304]{3,1,2,0:T(8,128)}), f32[16,8,1,2304]{3,1,2,0:T(8,128)S(1)}, u32[]{:S(2)}, u32[]{:S(2)}) async-start(f32[16,8,1,2304]{3,1,2,0:T(8,128)} %bitcast.8), calls=%async_computation.1 | async-start | bytes 2359296 | tf_op jit(solution)/shard_map/all_to_all | solution.py:26
  222.5 104.7 %all-gather.5.cloned.1.call-start = ((), (), s32[]{:S(2)}) async-start(), calls=%async_computation.6 | async-start | bytes 2396160 | tf_op jit(solution)/shard_map/all_gather | solution.py:55
  255.2 123.4 %copy-start = (bf16[512,1024]{1,0:T(8,128)(2,1)S(1)}, bf16[512,1024]{1,0:T(8,128)(2,1)}, u32[]{:S(2)}) copy-start(bf16[512,1024]{1,0:T(8,128)(2,1)} %all-reduce.3.cloned.1.call-done) | copy-start | bytes 3145732
  255.2 123.4 %all-reduce.5.cloned.1.call-start = ((), (), s32[]{:S(2)}) async-start(), calls=%async_computation.7 | async-start | bytes 2097152 | tf_op jit(solution)/shard_map/psum | solution.py:60
Sparse Core Ops, SparseCore 0:
  11.2 80.7 all-gather.2
  98.7 44.6 all-reduce.2
  255.3 71.8 all-gather.4
  334.1 44.5 all-reduce.4
where the time goes:
time: 499 us; the launch traced here: 498 us
  waiting for transfers between devices  277 us (56%)
  blocking collectives  159 us (32%)
  matrix products  23.2 us (5%)
  other arithmetic  14.9 us (3%)
  between operations  13.9 us (3%)
  starting transfers between devices  9.54 us (2%)
    all_to_all x2, blocking collectives, sent_and_summed(): parts = lax.all_to_all(split_up(array, dim, length), axis, 0, 0, tiled=True)  118 us
    all_gather x1, waiting for transfers between devices, shards(): lax.all_gather(activations, FEAT, axis=0, tiled=True)  84 us
    all_gather x1, waiting for transfers between devices, shards(): lax.all_gather(error.astype(jnp.bfloat16), FEAT, axis=0, tiled=True)  71.8 us
    psum x1, waiting for transfers between devices, shards(): lax.psum(partial_value.astype(jnp.bfloat16), 'layer').astype(jnp.float32)  44.8 us
    psum x1, waiting for transfers between devices, shards(): lax.psum(grad_part.astype(jnp.bfloat16), 'layer').astype(jnp.float32)  44.7 us
    all_to_all x1, blocking collectives, sum_by_axis(): lax.all_to_all(nearer, far, split_axis=0, concat_axis=0, tiled=True)  40.7 us
    all_to_all x1, waiting for transfers between devices, sum_by_axis(): lax.all_to_all(nearer, far, split_axis=0, concat_axis=0, tiled=True)  31 us
  transfers between devices with their start and end apart: 5, of which 5 were waited for; matrix products, arithmetic and copies ran while one was open for 0% of the time, Pallas kernels for 0%

commit v1 on v0

--- a/solution.py
+++ b/solution.py
@@ -31,7 +31,9 @@
     tok_dev = activations.shape[0]
     partial_value = jnp.einsum(
         "tld,ldf->tf",
-        lax.all_gather(activations, FEAT, axis=0, tiled=True),
+        jnp.concatenate(
+            lax.all_to_all(jnp.stack([activations] * lax.axis_size(FEAT)), FEAT, 0, 0), axis=0
+        ),
         enc_weight,
         preferred_element_type=jnp.float32,
     )

time: 499 us -> 480 us (0.962)
  waiting for transfers between devices: 277 us -> 188 us
  blocking collectives: 159 us -> 231 us
    all_gather x1 -> x0, waiting for transfers between devices: 84 us -> none  [shards(): lax.all_gather(activations, FEAT, axis=0, tiled=True)]
    all_to_all x0 -> x1, blocking collectives: none -> 72.8 us  [shards(): lax.all_to_all(jnp.stack([activations] * lax.axis_size(FEAT)), FEAT, 0, 0)]
  transfers between devices with their start and end apart: 5 -> 4, of which waited for: 5 -> 4; matrix products, arithmetic and copies ran while one was open for 0% -> 0% of each run, Pallas kernels for 0% -> 0%
where the time goes in v1:
time: 480 us
  blocking collectives  231 us (48%)
  waiting for transfers between devices  188 us (39%)
  matrix products  20.2 us (4%)
  other arithmetic  14.9 us (3%)
  between operations  13.8 us (3%)
  starting transfers between devices  9.5 us (2%)
    all_to_all x2, blocking collectives, sent_and_summed(): parts = lax.all_to_all(split_up(array, dim, length), axis, 0, 0, tiled=True)  118 us
    all_to_all x1, blocking collectives, shards(): lax.all_to_all(jnp.stack([activations] * lax.axis_size(FEAT)), FEAT, 0, 0)  72.8 us
    all_gather x1, waiting for transfers between devices, shards(): lax.all_gather(error.astype(jnp.bfloat16), FEAT, axis=0, tiled=True)  71.8 us
    psum x1, waiting for transfers between devices, shards(): lax.psum(grad_part.astype(jnp.bfloat16), 'layer').astype(jnp.float32)  44.8 us
    all_to_all x1, blocking collectives, sum_by_axis(): lax.all_to_all(nearer, far, split_axis=0, concat_axis=0, tiled=True)  40.7 us
    psum x1, waiting for transfers between devices, shards(): lax.psum(partial_value.astype(jnp.bfloat16), 'layer').astype(jnp.float32)  40.5 us
    all_to_all x1, waiting for transfers between devices, sum_by_axis(): lax.all_to_all(nearer, far, split_axis=0, concat_axis=0, tiled=True)  31 us
  transfers between devices with their start and end apart: 4, of which 4 were waited for; matrix products, arithmetic and copies ran while one was open for 0% of the time, Pallas kernels for 0%

profile of v1, /device:TPU:32, one launch (start us, length us, event | category | flops | bytes accessed | tf_op | source)
XLA Modules:
  0.0 479.7 jit_solution(17481629215664455904)
XLA Ops:
  7.2 0.9 stack.2
  8.1 72.8 %all_to_all.25 = bf16[64,8,1,2304]{3,1,2,0:T(8,128)(2,1)S(1)} all-to-all(bf16[64,8,1,2304]{3,1,2,0:T(8,128)(2,1)S(1)} %stack.2), channel_id=1, replica_groups=mesh['layer'=4,'feat_0'=4,'feat_1'=4,'feat_2'=4] {'feat_0','feat_1','fea..., dimensions={0} | all-to-all | bytes 4718592 | tf_op jit(solution)/shard_map/all_to_all | solution.py:35
  81.0 3.6 fusion.10
  84.5 40.5 %all-reduce.3.cloned.1.call-done = bf16[512,1024]{1,0:T(8,128)(2,1)} async-done(((bf16[512,1024]{1,0:T(8,128)(2,1)}), bf16[512,1024]{1,0:T(8,128)(2,1)}) %all-reduce.3.cloned.1.call-update) | async-done | bytes 1048592 | tf_op jit(solution)/shard_map/psum | solution.py:40
  125.0 1.9 fusion.9
  126.9 4.9 %convolution_bitcast_fusion.1 = f32[4,16,8,1,2304]{4,2,0,1,3:T(8,128)S(1)} fusion(bf16[16,4,8,1024]{3,2,1,0:T(8,128)(2,1)S(1)} %bitcast.67, bf16[1,1024,2304]{2,1,0:T(8,128)(2,1)} %param.9), kind=kOutput, calls=%fused_computation.1 | convolution fusion | flops 2415919104 | bytes 10485760 | tf_op jit(solution)/shard_map/tf,lfd->tld/dot_general | solution.py:47
  131.8 0.4 copy.10
  132.3 58.9 %all_to_all.26 = f32[4,16,8,1,2304]{4,2,1,3,0:T(8,128)} all-to-all(f32[4,16,8,1,2304]{4,2,1,3,0:T(8,128)S(1)} %copy.10), channel_id=1, replica_groups=mesh['layer'=4,'feat_0'=4,'feat_1'=4,'feat_2'=4] {'feat_2'}, dimensions={0} | all-to-all | bytes 9437184 | tf_op jit(solution)/shard_map/all_to_all | solution.py:18
  191.2 3.7 reduce_sum.53
  195.0 9.2 %all-to-all-start.2 = ((f32[16,8,1,2304]{3,1,2,0:T(8,128)}), f32[16,8,1,2304]{3,1,2,0:T(8,128)S(1)}, u32[]{:S(2)}, u32[]{:S(2)}) async-start(f32[16,8,1,2304]{3,1,2,0:T(8,128)} %bitcast.9), calls=%async_computation.2 | async-start | bytes 2359296 | tf_op jit(solution)/shard_map/all_to_all | solution.py:26
  204.3 0.8 dynamic-slice_convert_fusion
  205.0 31.0 %all-to-all-done.2 = f32[16,8,1,2304]{3,1,2,0:T(8,128)S(1)} async-done(((f32[16,8,1,2304]{3,1,2,0:T(8,128)}), f32[16,8,1,2304]{3,1,2,0:T(8,128)S(1)}, u32[]{:S(2)}, u32[]{:S(2)}) %all-to-all-start.2) | async-done | bytes 1179680 | tf_op jit(solution)/shard_map/all_to_all | solution.py:26
  236.1 0.7 fusion.23
  237.1 71.8 %all-gather.2.cloned.1.call-done = bf16[512,1,2304]{2,0,1:T(8,128)(2,1)} async-done(((bf16[8,1,2304]{2,0,1:T(8,128)(2,1)}), bf16[512,1,2304]{2,0,1:T(8,128)(2,1)}) %all-gather.2.cloned.1.call-update) | async-done | bytes 2359312 | tf_op jit(solution)/shard_map/all_gather | solution.py:57
  308.9 6.7 %fusion.15 = bf16[512,1024]{1,0:T(8,128)(2,1)} fusion(bf16[1,1024,2304]{2,1,0:T(8,128)(2,1)} %param.9, bf16[512,1,2304]{2,0,1:T(8,128)(2,1)} %all-gather.2.cloned.1.call-done), kind=kOutput, calls=%fused_computation.16 | convolution fusion | flops 2416443392 | bytes 8126464 | tf_op jit(solution)/shard_map/tld,lfd->tf/dot_general | solution.py:55
  315.6 44.8 %all-reduce.5.cloned.1.call-done = bf16[512,1024]{1,0:T(8,128)(2,1)} async-done(((bf16[512,1024]{1,0:T(8,128)(2,1)}), bf16[512,1024]{1,0:T(8,128)(2,1)}) %all-reduce.5.cloned.1.call-update) | async-done | bytes 1048592 | tf_op jit(solution)/shard_map/psum | solution.py:62
  360.3 3.6 multiply_convert_fusion
  364.0 5.0 %convolution_bitcast_fusion = f32[4,16,8,1,2304]{4,2,0,1,3:T(8,128)S(1)} fusion(bf16[16,4,8,1024]{3,2,1,0:T(8,128)(2,1)S(1)} %bitcast.66, bf16[1,2304,1024]{2,1,0:T(8,128)(2,1)} %param.8), kind=kOutput, calls=%fused_computation | convolution fusion | flops 2415919104 | bytes 10485760 | tf_op jit(solution)/shard_map/tf,ldf->tld/dot_general | solution.py:66
  369.0 0.4 copy.11
  369.4 58.9 %all_to_all.27 = f32[4,16,8,1,2304]{4,2,1,3,0:T(8,128)} all-to-all(f32[4,16,8,1,2304]{4,2,1,3,0:T(8,128)S(1)} %copy.11), channel_id=1, replica_groups=mesh['layer'=4,'feat_0'=4,'feat_1'=4,'feat_2'=4] {'feat_2'}, dimensions={0} | all-to-all | bytes 9437184 | tf_op jit(solution)/shard_map/all_to_all | solution.py:18
  428.3 2.7 reduce_sum.58
  431.0 40.7 %all_to_all.28 = f32[16,8,1,2304]{3,1,2,0:T(8,128)S(1)} all-to-all(f32[16,8,1,2304]{3,1,2,0:T(8,128)S(1)} %bitcast.65), channel_id=1, replica_groups=mesh['layer'=4,'feat_0'=4,'feat_1'=4,'feat_2'=4] {'feat_0','feat_1'}, dimensions={0} | all-to-all | bytes 2359296 | tf_op jit(solution)/shard_map/all_to_all | solution.py:26
  471.8 0.8 fusion.20
  472.6 0.5 multiply_bitcast_fusion
  (21 shorter events, 0.5 us)
Async XLA Ops:
  7.2 117.8 %all-reduce.3.cloned.1.call-start = ((), (), s32[]{:S(2)}) async-start(), calls=%async_computation.5 | async-start | bytes 2097152 | tf_op jit(solution)/shard_map/psum | solution.py:40
  8.1 72.8 %copy-start.5 = (bf16[1,2304,1024]{2,1,0:T(8,128)(2,1)S(1)}, bf16[1,2304,1024]{2,1,0:T(8,128)(2,1)}, u32[]{:S(2)}) copy-start(bf16[1,2304,1024]{2,1,0:T(8,128)(2,1)} %param.8) | copy-start | bytes 14155780
  80.9 44.1 %copy-start.2 = (f32[1024]{0:T(1024)S(1)}, f32[1024]{0:T(1024)}, u32[]{:S(2)}) copy-start(f32[1024]{0:T(1024)} %param.11) | copy-start | bytes 12292
  80.9 44.1 %copy-start.3 = (f32[1024]{0:T(1024)S(1)}, f32[1024]{0:T(1024)}, u32[]{:S(2)}) copy-start(f32[1024]{0:T(1024)} %param.10) | copy-start | bytes 12292
  194.9 9.3 %copy-start.4 = (f32[1,2304]{1,0:T(1,128)S(1)}, f32[1,2304]{1,0:T(1,128)}, u32[]{:S(2)}) copy-start(f32[1,2304]{1,0:T(1,128)} %param.12) | copy-start | bytes 27652
  195.0 41.2 %copy-start.1 = (bf16[8,1,2304]{2,0,1:T(8,128)(2,1)S(1)}, bf16[8,1,2304]{2,0,1:T(8,128)(2,1)}, u32[]{:S(2)}) copy-start(bf16[8,1,2304]{2,0,1:T(8,128)(2,1)} %param.7) | copy-start | bytes 110596
  195.0 41.1 %all-to-all-start.2 = ((f32[16,8,1,2304]{3,1,2,0:T(8,128)}), f32[16,8,1,2304]{3,1,2,0:T(8,128)S(1)}, u32[]{:S(2)}, u32[]{:S(2)}) async-start(f32[16,8,1,2304]{3,1,2,0:T(8,128)} %bitcast.9), calls=%async_computation.2 | async-start | bytes 2359296 | tf_op jit(solution)/shard_map/all_to_all | solution.py:26
  204.2 104.7 %all-gather.2.cloned.1.call-start = ((), (), s32[]{:S(2)}) async-start(), calls=%async_computation.6 | async-start | bytes 2396160 | tf_op jit(solution)/shard_map/all_gather | solution.py:57
  236.9 123.5 %copy-start = (bf16[512,1024]{1,0:T(8,128)(2,1)S(1)}, bf16[512,1024]{1,0:T(8,128)(2,1)}, u32[]{:S(2)}) copy-start(bf16[512,1024]{1,0:T(8,128)(2,1)} %all-reduce.3.cloned.1.call-done) | copy-start | bytes 3145732
  236.9 123.5 %all-reduce.5.cloned.1.call-start = ((), (), s32[]{:S(2)}) async-start(), calls=%async_computation.7 | async-start | bytes 2097152 | tf_op jit(solution)/shard_map/psum | solution.py:62
Sparse Core Ops, SparseCore 0:
  84.7 40.2 all-reduce.2
  237.0 71.8 all-gather.1
  315.7 44.6 all-reduce.4
